TPU v7x, 256 devices: a whole 4x4x8 slice. The times are simulated.
256 devices in a mesh: tok: 8 (over x, core), voc: 32 (over z, y).
Axes of the slice: x: 4, y: 4, z: 8, core: 2. Of those that a mesh axis runs over, the one named last changes fastest.
Arguments:
- hidden_rows: bfloat16 [1024, 8192], P('tok', 'voc'), may hold values from -2 to 2
- teacher_weight: bfloat16 [8192, 152064], P(None, ('tok', 'voc')), may hold values from -64 to 64
- student_logits: bfloat16 [1024, 128256], P('tok', 'voc'), may hold values from -8 to 300
- slot_source: int32 [32, 32, 256], P('voc'), may hold values from -1 to 4751, as said below
- slot_target: int32 [32, 32, 256], P('voc'), may hold values from -1 to 4007, as said below
Outputs:
- loss: float32 [1024], P('tok')
- student_grad: bfloat16 [1024, 128256], P('tok', 'voc')
Inputs may be any that keep to these rules, and one draw needn't show every extreme that they name: Each of the 4752 local columns of group g appears in exactly one slot of slot_source[g]; all other slots hold -1. One owner's 256 slots are filled in every group. slot_target[j, g, c] is -1 exactly where slot_source[g, j, c] is -1.
All inputs are finite; a program needn't handle non-finite values.
Results may differ from a plain program's by a relative error of at most 0.0022.
The roundings to bfloat16 on the way count: a program that leaves them out, or rounds other values in their place, can miss the bound.
Values may be sent and summed in bfloat16 or wider, within the bound.
No kernel may reach another device: no remote copies, remote signals or barrier semaphores. Data moves between devices by JAX's collectives and lax.ppermute only.
A program may use at most 128 MiB of HBM per device.

v0:
```python
import jax
import jax.numpy as jnp
from jax import lax
from jax.sharding import Mesh
from jax.sharding import PartitionSpec as P

VOC = ("voc_0", "voc_1")
TOK = ("tok_0", "tok_1")
TOK_VOC = ("tok_0", "tok_1", "voc_0", "voc_1")


def gathered_by_axis(value, axes, dim):
    if not axes:
        return value
    nearer = lax.all_gather(value, axes[-1], axis=dim, tiled=True)
    return gathered_by_axis(nearer, axes[:-1], dim)


def collected_together(value, axis):
    leaves = jax.tree.leaves(value)
    order = sorted(range(len(leaves)), key=lambda k: -leaves[k].size)
    width = (1, *leaves[order[0]].shape)[-1]
    lines = [
        jnp.pad(leaves[k].reshape(-1), (0, -leaves[k].size % width)).reshape(-1, width)
        for k in order
    ]
    both, at, found = (lax.all_gather(jnp.concatenate(lines), axis), 0, {})
    for k, line in zip(order, lines):
        slab = both[:, at : at + len(line)].reshape(len(both), -1)
        found[k] = slab[:, : leaves[k].size].reshape(-1, *leaves[k].shape)
        at += len(line)
    numbers = iter(range(len(leaves)))
    return jax.tree.map(lambda _: found[next(numbers)], value)


def joined_all(value, axes, combine):
    for axis in axes:
        pieces = collected_together(value, axis)
        value = jax.tree.map(lambda part: part[0], pieces)
        for k in range(1, lax.axis_size(axis)):
            value = combine(value, jax.tree.map(lambda part: part[k], pieces))
    return value


def copy_for_each(value, axis):
    copies = jnp.broadcast_to(value, (lax.axis_size(axis), *value.shape))
    return lax.all_to_all(copies, axis, split_axis=0, concat_axis=0, tiled=True)


def gathered_once(value, axis):
    leaves = jax.tree.leaves(value)
    order = sorted(range(len(leaves)), key=lambda k: -leaves[k].size)
    width = (1, *leaves[order[0]].shape)[-1]
    lines = [
        jnp.pad(leaves[k].reshape(-1), (0, -leaves[k].size % width)).reshape(-1, width)
        for k in order
    ]
    both, at, found = (copy_for_each(jnp.concatenate(lines), axis), 0, {})
    for k, line in zip(order, lines):
        slab = both[:, at : at + len(line)].reshape(len(both), -1)
        found[k] = slab[:, : leaves[k].size].reshape(-1, *leaves[k].shape)
        at += len(line)
    numbers = iter(range(len(leaves)))
    return jax.tree.map(lambda _: found[next(numbers)], value)


def combined_pairwise(pieces, combine):
    while len(jax.tree.leaves(pieces)[0]) > 1:
        pieces = jax.vmap(combine)(
            *(jax.tree.map(lambda part: part[side::2], pieces) for side in (0, 1))
        )
    return jax.tree.map(lambda part: part[0], pieces)


def combined_all(value, axis, combine):
    pieces = gathered_once(value, axis)
    return combined_pairwise(pieces, combine)


def teacher_combine(first, second):
    highest = jnp.maximum(first[0], second[0])
    summed = first[1] * jnp.exp(first[0] - highest) + second[1] * jnp.exp(second[0] - highest)
    return (highest, summed)


def student_combine(first, second):
    highest = jnp.maximum(first[0], second[0])
    summed = first[1] * jnp.exp(first[0] - highest) + second[1] * jnp.exp(second[0] - highest)
    return (highest, summed, first[2] + second[2], first[3] + second[3])


def shards(hidden_rows, teacher_weight, student_logits, slot_source, slot_target):
    full_rows = gathered_by_axis(hidden_rows, VOC, 1)
    logits = jnp.dot(
        lax.all_gather(full_rows, TOK, axis=0, tiled=True),
        teacher_weight,
        preferred_element_type=jnp.float32,
    )
    local_max = jnp.max(logits, axis=1)
    shifted_local = jnp.exp(logits - local_max[:, None])
    teacher_max, teacher_total = joined_all(
        (local_max, jnp.sum(shifted_local, axis=1)), TOK_VOC, teacher_combine
    )
    shifted = shifted_local * jnp.exp(local_max - teacher_max)[:, None]
    probs = (shifted / teacher_total[:, None]).astype(jnp.bfloat16)
    grouped = lax.all_to_all(probs, TOK, split_axis=0, concat_axis=1, tiled=True)
    source = slot_source[0]
    flat_source = source.reshape(-1)
    picked = jnp.take(grouped, jnp.maximum(flat_source, 0), axis=1)
    picked = jnp.where((flat_source >= 0)[None, :], picked, jnp.zeros_like(picked))
    outgoing = picked.reshape(grouped.shape[0], source.shape[0], source.shape[1])
    width = student_logits.shape[1]
    target = slot_target[0].reshape(-1)
    column = jnp.where(target >= 0, target, width)
    arrived = lax.all_to_all(outgoing, VOC, split_axis=1, concat_axis=1, tiled=True)
    values = arrived.reshape(arrived.shape[0], -1).astype(jnp.float32)
    folded = (
        jnp.zeros((arrived.shape[0], width), jnp.float32).at[:, column].add(values, mode="drop")
    )
    student = student_logits.astype(jnp.float32)
    own_max = jnp.max(student, axis=1)
    own_total = jnp.sum(jnp.exp(student - own_max[:, None]), axis=1)
    cross = jnp.sum(folded * student, axis=1)
    weight_mass = jnp.sum(folded, axis=1)
    student_max, student_total, cross, weight_mass = combined_all(
        (own_max, own_total, cross, weight_mass), VOC, student_combine
    )
    student_lse = student_max + jnp.log(student_total)
    loss = student_lse * weight_mass - cross
    student_grad = (jnp.exp(student - student_lse[:, None]) - folded).astype(jnp.bfloat16)
    return (loss, student_grad)


def solution(mesh):
    finer = Mesh(mesh.devices.reshape(4, 2, 8, 4), ("tok_0", "tok_1", "voc_0", "voc_1"))
    placed = (P(TOK, VOC), P(None, TOK_VOC), P(TOK, VOC), P(VOC, None, None), P(VOC, None, None))
    return jax.shard_map(
        shards, mesh=finer, in_specs=placed, out_specs=(P(TOK), P(TOK, VOC)), check_vma=False
    )
```

profile of v0, /device:TPU:2, one launch (start us, length us, event | category | flops | bytes accessed | tf_op | source)
XLA Modules:
  0.0 400.6 jit_solution(5841360051451919552)
XLA Ops:
  7.2 0.0 all-gather.11.cloned.1.call-start
  7.2 14.5 %all_gather.33 = bf16[128,1024]{1,0:T(8,128)(2,1)} all-gather(bf16[128,256]{1,0:T(8,128)(2,1)} %param.5), channel_id=1, replica_groups=mesh['tok_0'=4,'tok_1'=2,'voc_0'=8,'voc_1'=4] {'voc_1'}, dimensions={1}, use_global_device_ids=true | all-gather | bytes 327680 | tf_op jit(solution)/shard_map/all_gather | solution.py:15
  21.7 0.0 all-gather.11.cloned.1.call-update
  21.7 0.0 all-gather.13.cloned.1.call-start
  21.7 42.5 %all-gather.11.cloned.1.call-done = bf16[128,8192]{1,0:T(8,128)(2,1)} async-done(((bf16[128,1024]{1,0:T(8,128)(2,1)}), bf16[128,8192]{1,0:T(8,128)(2,1)}) %all-gather.11.cloned.1.call-update) | async-done | bytes 2097168 | tf_op jit(solution)/shard_map/all_gather | solution.py:15
  64.2 0.0 all-gather.13.cloned.1.call-update
  64.3 87.5 %all-gather.13.cloned.1.call-done = bf16[1024,8192]{1,0:T(8,128)(2,1)} async-done(((bf16[128,8192]{1,0:T(8,128)(2,1)}), bf16[1024,8192]{1,0:T(8,128)(2,1)}) %all-gather.13.cloned.1.call-update) | async-done | bytes 16777232 | tf_op jit(solution)/shard_map/all_gather | solution.py:95
  151.7 15.5 %fusion.61 = (f32[1024]{0:T(1024)S(1)}, f32[1024,594]{0,1:T(8,128)S(1)}) fusion(bf16[1024,8192]{1,0:T(8,128)(2,1)} %all-gather.13.cloned.1.call-done, bf16[8192,594]{0,1:T(8,128)(2,1)} %param.6), kind=kOutput, calls=%fused_computation.118 | convolution fusion | flops 9966273536 | bytes 28946432 | tf_op jit(solution)/shard_map/dot_general | solution.py:94
  167.3 0.4 fusion.1
  167.7 10.8 %all-gather.4 = f32[4,2,1024]{2,1,0:T(2,128)S(1)} all-gather(f32[1,2,1024]{2,1,0:T(2,128)S(1)} %maximum_bitcast_fusion.1), channel_id=2, replica_groups=mesh['tok_0'=4,'tok_1'=2,'voc_0'=8,'voc_1'=4] {'tok_0'}, dimensions={0}, use_global_device_ids=true | all-gather | bytes 40960 | tf_op jit(solution)/shard_map/all_gather | solution.py:27
  178.5 0.1 fusion.34
  178.5 1.8 all-gather.5
  180.4 26.3 %all-gather.6 = f32[8,2,1024]{2,1,0:T(2,128)S(1)} all-gather(f32[1,2,1024]{2,1,0:T(2,128)S(1)} %maximum_bitcast_fusion.3), channel_id=4, replica_groups=mesh['tok_0'=4,'tok_1'=2,'voc_0'=8,'voc_1'=4] {'voc_0'}, dimensions={0}, use_global_device_ids=true | all-gather | bytes 73728 | tf_op jit(solution)/shard_map/all_gather | solution.py:27
  206.7 0.1 fusion.10
  206.8 12.3 %all-gather.7 = f32[4,2,1024]{2,1,0:T(2,128)S(1)} all-gather(f32[1,2,1024]{2,1,0:T(2,128)S(1)} %maximum_bitcast_fusion.4), channel_id=5, replica_groups=mesh['tok_0'=4,'tok_1'=2,'voc_0'=8,'voc_1'=4] {'voc_1'}, dimensions={0}, use_global_device_ids=true | all-gather | bytes 40960 | tf_op jit(solution)/shard_map/all_gather | solution.py:27
  219.1 0.5 divide_convert_fusion
  219.6 0.3 copy.13
  219.9 0.1 slice_bitcast_fusion
  220.0 0.0 copy-start.1
  220.0 1.2 copy.9
  221.2 5.3 %all-to-all-start = ((bf16[8,128,594]{1,2,0:T(8,128)(2,1)}), bf16[8,128,594]{1,2,0:T(8,128)(2,1)S(1)}, u32[]{:S(2)}, u32[]{:S(2)}) async-start(bf16[8,128,594]{1,2,0:T(8,128)(2,1)} %copy.9), calls=%async_computation | async-start | bytes 2457600 | tf_op jit(solution)/shard_map/all_to_all | solution.py:106
  226.5 0.0 copy-done.1
  226.6 16.4 %all-to-all-done = bf16[8,128,594]{1,2,0:T(8,128)(2,1)S(1)} async-done(((bf16[8,128,594]{1,2,0:T(8,128)(2,1)}), bf16[8,128,594]{1,2,0:T(8,128)(2,1)S(1)}, u32[]{:S(2)}, u32[]{:S(2)}) %all-to-all-start) | async-done | bytes 1216544 | tf_op jit(solution)/shard_map/all_to_all | solution.py:106
  242.9 0.4 all_to_all.23
  243.3 24.0 %gather_fusion = bf16[8192,128]{1,0:T(8,128)(2,1)S(1)} fusion(bf16[128,4752]{0,1:T(8,128)(2,1)S(1)} %all_to_all.23, s32[8192]{0:T(1024)S(1)} %broadcast_clamp_fusion), kind=kCustom, calls=%fused_computation | custom fusion | bytes 4227072 | tf_op jit(solution)/shard_map/jit(_take)/gather | solution.py:109
  267.3 4.6 %select_select_fusion = bf16[128,32,256]{0,2,1:T(8,128)(2,1)} fusion(bf16[128,32,256]{0,2,1:T(8,128)(2,1)S(1)} %bitcast.322, pred[32,256]{1,0:T(8,128)(4,1)S(1)} %get-tuple-element.26, pred[32,256]{1,0:T(8,128)(4,1)S(1)} %get-tuple-element.25), kind=kLoop, calls=%fused_computation.10 | loop fusion | flops 2097152 | bytes 4210688 | tf_op jit(solution)/shard_map/jit(_where)/select_n | solution.py:110
  271.9 0.0 copy-start.2
  271.9 0.0 copy-start
  271.9 8.0 %all-to-all-start.1 = ((bf16[128,32,256]{0,2,1:T(8,128)(2,1)}), bf16[128,32,256]{0,2,1:T(8,128)(2,1)}, u32[]{:S(2)}, u32[]{:S(2)}) async-start(bf16[128,32,256]{0,2,1:T(8,128)(2,1)} %select_select_fusion), calls=%async_computation.1 | async-start | bytes 4194304 | tf_op jit(solution)/shard_map/all_to_all | solution.py:115
  280.0 0.0 copy-done.2
  280.0 0.0 copy-done
  280.0 0.5 reduce_max.27
  280.6 0.1 compare_select_fusion
  280.6 49.2 %all-to-all-done.1 = bf16[128,32,256]{0,2,1:T(8,128)(2,1)} async-done(((bf16[128,32,256]{0,2,1:T(8,128)(2,1)}), bf16[128,32,256]{0,2,1:T(8,128)(2,1)}, u32[]{:S(2)}, u32[]{:S(2)}) %all-to-all-start.1) | async-done | bytes 2097184 | tf_op jit(solution)/shard_map/all_to_all | solution.py:115
  329.8 45.0 %scatter_custom_fusion = f32[128,4008]{0,1:T(8,128)S(1)} fusion(s32[8192]{0:T(1024)S(1)} %bitcast.338, bf16[128,8192]{0,1:T(8,128)(2,1)} %bitcast.62, f32[]{:T(128)} %constant.10.clone.1), kind=kCustom, calls=%fused_computation.3 | custom fusion | flops 2097152 | bytes 4149252 | tf_op jit(solution)/shard_map/scatter-add | solution.py:118
  374.9 0.6 fusion.4
  375.4 15.7 %all_to_all.29 = f32[32,4,128]{2,1,0:T(4,128)S(1)} all-to-all(f32[32,4,128]{2,1,0:T(4,128)S(1)} %broadcast_in_dim.44), channel_id=1, replica_groups=mesh['tok_0'=4,'tok_1'=2,'voc_0'=8,'voc_1'=4] {'voc_0','voc_1'}, dimensions={0} | all-to-all | bytes 131072 | tf_op jit(solution)/shard_map/all_to_all | solution.py:47
  391.9 0.5 bitcast_subtract_fusion
  392.4 1.4 fusion.7
  (60 shorter events, 0.9 us)
Async XLA Ops:
  7.2 57.1 %all-gather.11.cloned.1.call-start = ((), (), s32[]{:S(2)}) async-start(), calls=%async_computation.3 | async-start | bytes 2359296 | tf_op jit(solution)/shard_map/all_gather | solution.py:15
  21.7 130.0 %all-gather.13.cloned.1.call-start = ((), (), s32[]{:S(2)}) async-start(), calls=%async_computation.4 | async-start | bytes 18874368 | tf_op jit(solution)/shard_map/all_gather | solution.py:95
  220.0 6.5 %copy-start.1 = (s32[1,32,256]{2,1,0:T(8,128)S(1)}, s32[1,32,256]{2,1,0:T(8,128)}, u32[]{:S(2)}) copy-start(s32[1,32,256]{2,1,0:T(8,128)} %param.8) | copy-start | bytes 98308
  221.2 21.7 %all-to-all-start = ((bf16[8,128,594]{1,2,0:T(8,128)(2,1)}), bf16[8,128,594]{1,2,0:T(8,128)(2,1)S(1)}, u32[]{:S(2)}, u32[]{:S(2)}) async-start(bf16[8,128,594]{1,2,0:T(8,128)(2,1)} %copy.9), calls=%async_computation | async-start | bytes 2457600 | tf_op jit(solution)/shard_map/all_to_all | solution.py:106
  271.9 8.1 %copy-start.2 = (s32[1,32,256]{2,1,0:T(8,128)S(1)}, s32[1,32,256]{2,1,0:T(8,128)}, u32[]{:S(2)}) copy-start(s32[1,32,256]{2,1,0:T(8,128)} %param.9) | copy-start | bytes 98308
  271.9 8.1 %copy-start = (bf16[128,4008]{0,1:T(8,128)(2,1)S(1)}, bf16[128,4008]{0,1:T(8,128)(2,1)}, u32[]{:S(2)}) copy-start(bf16[128,4008]{0,1:T(8,128)(2,1)} %param.7) | copy-start | bytes 3078148
  271.9 57.9 %all-to-all-start.1 = ((bf16[128,32,256]{0,2,1:T(8,128)(2,1)}), bf16[128,32,256]{0,2,1:T(8,128)(2,1)}, u32[]{:S(2)}, u32[]{:S(2)}) async-start(bf16[128,32,256]{0,2,1:T(8,128)(2,1)} %select_select_fusion), calls=%async_computation.1 | async-start | bytes 4194304 | tf_op jit(solution)/shard_map/all_to_all | solution.py:115
Sparse Core Ops, SparseCore 0:
  21.8 42.3 all-gather.10
  66.1 85.6 all-gather.12
where the time goes:
time: 401 us
  waiting for transfers between devices  196 us (49%)
  blocking collectives  81.3 us (20%)
  other arithmetic  53.9 us (13%)
  local copies, waits for them, and re-layouts  26.6 us (7%)
  matrix products  15.5 us (4%)
  between operations  14.3 us (4%)
  starting transfers between devices  13.4 us (3%)
    all_gather x1, waiting for transfers between devices, shards(): lax.all_gather(full_rows, TOK, axis=0, tiled=True)  87.5 us
    all_gather x4, blocking collectives, collected_together(): both, at, found = (lax.all_gather(jnp.concatenate(lines), axis), 0, {})  51.1 us
    all_to_all x1, waiting for transfers between devices, shards(): lax.all_to_all(outgoing, VOC, split_axis=1, concat_axis=1, tiled=True)  49.2 us
    scatter-add x1, other arithmetic, shards(): jnp.zeros((arrived.shape[0], width), jnp.float32).at[:, column]  45 us
    all_gather x1, waiting for transfers between devices, gathered_by_axis(): nearer = lax.all_gather(value, axes[-1], axis=dim, tiled=True)  42.5 us
    gather x1, local copies, waits for them, and re-layouts, shards(): picked = jnp.take(grouped, jnp.maximum(flat_source, 0), axis=1)  24 us
    all_to_all x1, waiting for transfers between devices, shards(): lax.all_to_all(probs, TOK, split_axis=0, concat_axis=1, tiled=True)  16.4 us
    all_to_all x1, blocking collectives, copy_for_each(): return lax.all_to_all(copies, axis, split_axis=0, concat_axis=0, tiled=True)  15.7 us
  transfers between devices with their start and end apart: 4, of which 4 were waited for; matrix products, arithmetic and copies ran while one was open for 0% of the time, Pallas kernels for 0%

commit v1 on v0

--- a/solution.py
+++ b/solution.py
@@ -92,7 +92,9 @@
 def shards(hidden_rows, teacher_weight, student_logits, slot_source, slot_target):
     full_rows = gathered_by_axis(hidden_rows, VOC, 1)
     logits = jnp.dot(
-        lax.all_gather(full_rows, TOK, axis=0, tiled=True),
+        jnp.concatenate(
+            lax.all_to_all(jnp.stack([full_rows] * lax.axis_size(TOK)), TOK, 0, 0), axis=0
+        ),
         teacher_weight,
         preferred_element_type=jnp.float32,
     )

time: 401 us -> 507 us (1.26)
  blocking collectives: 81.3 us -> 270 us
  waiting for transfers between devices: 196 us -> 108 us
    all_to_all x0 -> x1, blocking collectives: none -> 190 us  [shards(): lax.all_to_all(jnp.stack([full_rows] * lax.axis_size(TOK)), TOK, 0, 0)]
    all_gather x1 -> x0, waiting for transfers between devices: 87.5 us -> none  [shards(): lax.all_gather(full_rows, TOK, axis=0, tiled=True)]
  transfers between devices with their start and end apart: 4 -> 3, of which waited for: 4 -> 3; matrix products, arithmetic and copies ran while one was open for 0% -> 0% of each run, Pallas kernels for 0% -> 0%
where the time goes in v1:
time: 507 us; the launch traced here: 506 us
  blocking collectives  270 us (53%)
  waiting for transfers between devices  108 us (21%)
  other arithmetic  53.9 us (11%)
  local copies, waits for them, and re-layouts  30.4 us (6%)
  matrix products  18.8 us (4%)
  between operations  14.3 us (3%)
  starting transfers between devices  11.3 us (2%)
    all_to_all x1, blocking collectives, shards(): lax.all_to_all(jnp.stack([full_rows] * lax.axis_size(TOK)), TOK, 0, 0)  190 us
    all_gather x4, blocking collectives, collected_together(): both, at, found = (lax.all_gather(jnp.concatenate(lines), axis), 0, {})  49.4 us
    all_to_all x1, waiting for transfers between devices, shards(): lax.all_to_all(outgoing, VOC, split_axis=1, concat_axis=1, tiled=True)  49.2 us
    scatter-add x1, other arithmetic, shards(): jnp.zeros((arrived.shape[0], width), jnp.float32).at[:, column]  45 us
    all_gather x1, waiting for transfers between devices, gathered_by_axis(): nearer = lax.all_gather(value, axes[-1], axis=dim, tiled=True)  42.5 us
    gather x1, local copies, waits for them, and re-layouts, shards(): picked = jnp.take(grouped, jnp.maximum(flat_source, 0), axis=1)  24 us
    dot_general x1, matrix products, shards(): jnp.dot(jnp.concatenate(lax.all_to_all(jnp.stack([full_rows] * lax.axis_s...  18.8 us
    all_to_all x1, waiting for transfers between devices, shards(): lax.all_to_all(probs, TOK, split_axis=0, concat_axis=1, tiled=True)  16.3 us
  transfers between devices with their start and end apart: 3, of which 3 were waited for; matrix products, arithmetic and copies ran while one was open for 0% of the time, Pallas kernels for 0%

profile of v1, /device:TPU:2, one launch (start us, length us, event | category | flops | bytes accessed | tf_op | source)
XLA Modules:
  0.0 506.4 jit_solution(9828562998895494294)
XLA Ops:
  7.2 0.0 all-gather.10.cloned.1.call-start
  7.2 14.5 %all_gather.30 = bf16[128,1024]{1,0:T(8,128)(2,1)} all-gather(bf16[128,256]{1,0:T(8,128)(2,1)} %param.5), channel_id=1, replica_groups=mesh['tok_0'=4,'tok_1'=2,'voc_0'=8,'voc_1'=4] {'voc_1'}, dimensions={1}, use_global_device_ids=true | all-gather | bytes 327680 | tf_op jit(solution)/shard_map/all_gather | solution.py:15
  21.7 0.0 all-gather.10.cloned.1.call-update
  21.7 42.5 %all-gather.10.cloned.1.call-done = bf16[128,8192]{1,0:T(8,128)(2,1)} async-done(((bf16[128,1024]{1,0:T(8,128)(2,1)}), bf16[128,8192]{1,0:T(8,128)(2,1)}) %all-gather.10.cloned.1.call-update) | async-done | bytes 2097168 | tf_op jit(solution)/shard_map/all_gather | solution.py:15
  64.2 3.8 stack.2
  68.0 190.0 %all_to_all.34 = bf16[8,128,8192]{2,1,0:T(8,128)(2,1)S(1)} all-to-all(bf16[8,128,8192]{2,1,0:T(8,128)(2,1)S(1)} %stack.2), channel_id=1, replica_groups=mesh['tok_0'=4,'tok_1'=2,'voc_0'=8,'voc_1'=4] {'tok_0','tok_1'}, dimensions={0} | all-to-all | bytes 33554432 | tf_op jit(solution)/shard_map/all_to_all | solution.py:96
  258.0 18.8 %fusion.61 = (f32[1024]{0:T(1024)S(1)}, f32[1024,594]{0,1:T(8,128)S(1)}) fusion(bf16[1024,8192]{1,0:T(8,128)(2,1)S(1)} %bitcast.323, bf16[8192,594]{0,1:T(8,128)(2,1)} %param.6), kind=kOutput, calls=%fused_computation.118 | convolution fusion | flops 9966273536 | bytes 28946432 | tf_op jit(solution)/shard_map/dot_general | solution.py:94
  276.8 0.4 fusion.1
  277.2 10.7 %all-gather.4 = f32[4,2,1024]{2,1,0:T(2,128)S(1)} all-gather(f32[1,2,1024]{2,1,0:T(2,128)S(1)} %maximum_bitcast_fusion.1), channel_id=2, replica_groups=mesh['tok_0'=4,'tok_1'=2,'voc_0'=8,'voc_1'=4] {'tok_0'}, dimensions={0}, use_global_device_ids=true | all-gather | bytes 40960 | tf_op jit(solution)/shard_map/all_gather | solution.py:27
  287.9 0.1 fusion.34
  288.0 1.8 all-gather.5
  289.8 24.6 %all-gather.6 = f32[8,2,1024]{2,1,0:T(2,128)S(1)} all-gather(f32[1,2,1024]{2,1,0:T(2,128)S(1)} %maximum_bitcast_fusion.3), channel_id=4, replica_groups=mesh['tok_0'=4,'tok_1'=2,'voc_0'=8,'voc_1'=4] {'voc_0'}, dimensions={0}, use_global_device_ids=true | all-gather | bytes 73728 | tf_op jit(solution)/shard_map/all_gather | solution.py:27
  314.4 0.1 fusion.10
  314.5 12.3 %all-gather.7 = f32[4,2,1024]{2,1,0:T(2,128)S(1)} all-gather(f32[1,2,1024]{2,1,0:T(2,128)S(1)} %maximum_bitcast_fusion.4), channel_id=5, replica_groups=mesh['tok_0'=4,'tok_1'=2,'voc_0'=8,'voc_1'=4] {'voc_1'}, dimensions={0}, use_global_device_ids=true | all-gather | bytes 40960 | tf_op jit(solution)/shard_map/all_gather | solution.py:27
  326.9 0.5 divide_convert_fusion
  327.3 0.3 copy.13
  327.7 0.1 slice_bitcast_fusion
  327.8 0.0 copy-start.1
  327.8 1.2 copy.9
  329.0 4.5 all-to-all-start.1
  333.5 0.0 copy-done.1
  333.6 16.3 %all-to-all-done.1 = bf16[8,128,594]{1,2,0:T(8,128)(2,1)S(1)} async-done(((bf16[8,128,594]{1,2,0:T(8,128)(2,1)}), bf16[8,128,594]{1,2,0:T(8,128)(2,1)S(1)}, u32[]{:S(2)}, u32[]{:S(2)}) %all-to-all-start.1) | async-done | bytes 1216544 | tf_op jit(solution)/shard_map/all_to_all | solution.py:108
  349.9 0.4 all_to_all.27
  350.3 24.0 %gather_fusion = bf16[8192,128]{1,0:T(8,128)(2,1)S(1)} fusion(bf16[128,4752]{0,1:T(8,128)(2,1)S(1)} %all_to_all.27, s32[8192]{0:T(1024)S(1)} %broadcast_clamp_fusion), kind=kCustom, calls=%fused_computation | custom fusion | bytes 4227072 | tf_op jit(solution)/shard_map/jit(_take)/gather | solution.py:111
  374.3 4.6 select_select_fusion
  378.9 0.0 copy-start.2
  378.9 0.0 copy-start
  378.9 6.8 %all-to-all-start.2 = ((bf16[128,32,256]{0,2,1:T(8,128)(2,1)}), bf16[128,32,256]{0,2,1:T(8,128)(2,1)}, u32[]{:S(2)}, u32[]{:S(2)}) async-start(bf16[128,32,256]{0,2,1:T(8,128)(2,1)} %select_select_fusion), calls=%async_computation.2 | async-start | bytes 4194304 | tf_op jit(solution)/shard_map/all_to_all | solution.py:117
  385.7 0.0 copy-done.2
  385.7 0.0 copy-done
  385.8 0.5 reduce_max.27
  386.3 0.1 compare_select_fusion
  386.4 49.2 %all-to-all-done.2 = bf16[128,32,256]{0,2,1:T(8,128)(2,1)} async-done(((bf16[128,32,256]{0,2,1:T(8,128)(2,1)}), bf16[128,32,256]{0,2,1:T(8,128)(2,1)}, u32[]{:S(2)}, u32[]{:S(2)}) %all-to-all-start.2) | async-done | bytes 2097184 | tf_op jit(solution)/shard_map/all_to_all | solution.py:117
  435.5 45.0 %scatter_custom_fusion = f32[128,4008]{0,1:T(8,128)S(1)} fusion(s32[8192]{0:T(1024)S(1)} %bitcast.340, bf16[128,8192]{0,1:T(8,128)(2,1)} %bitcast.63, f32[]{:T(128)} %constant.10.clone.1), kind=kCustom, calls=%fused_computation.3 | custom fusion | flops 2097152 | bytes 4149252 | tf_op jit(solution)/shard_map/scatter-add | solution.py:120
  480.6 0.6 fusion.4
  481.2 15.7 %all_to_all.35 = f32[32,4,128]{2,1,0:T(4,128)S(1)} all-to-all(f32[32,4,128]{2,1,0:T(4,128)S(1)} %broadcast_in_dim.44), channel_id=1, replica_groups=mesh['tok_0'=4,'tok_1'=2,'voc_0'=8,'voc_1'=4] {'voc_0','voc_1'}, dimensions={0} | all-to-all | bytes 131072 | tf_op jit(solution)/shard_map/all_to_all | solution.py:47
  497.6 0.5 bitcast_subtract_fusion
  498.1 1.4 fusion.7
  (60 shorter events, 0.9 us)
Async XLA Ops:
  7.2 57.1 %all-gather.10.cloned.1.call-start = ((), (), s32[]{:S(2)}) async-start(), calls=%async_computation.4 | async-start | bytes 2359296 | tf_op jit(solution)/shard_map/all_gather | solution.py:15
  327.8 5.7 %copy-start.1 = (s32[1,32,256]{2,1,0:T(8,128)S(1)}, s32[1,32,256]{2,1,0:T(8,128)}, u32[]{:S(2)}) copy-start(s32[1,32,256]{2,1,0:T(8,128)} %param.8) | copy-start | bytes 98308
  329.0 20.9 %all-to-all-start.1 = ((bf16[8,128,594]{1,2,0:T(8,128)(2,1)}), bf16[8,128,594]{1,2,0:T(8,128)(2,1)S(1)}, u32[]{:S(2)}, u32[]{:S(2)}) async-start(bf16[8,128,594]{1,2,0:T(8,128)(2,1)} %copy.9), calls=%async_computation.1 | async-start | bytes 2457600 | tf_op jit(solution)/shard_map/all_to_all | solution.py:108
  378.9 6.8 %copy-start.2 = (s32[1,32,256]{2,1,0:T(8,128)S(1)}, s32[1,32,256]{2,1,0:T(8,128)}, u32[]{:S(2)}) copy-start(s32[1,32,256]{2,1,0:T(8,128)} %param.9) | copy-start | bytes 98308
  378.9 6.8 %copy-start = (bf16[128,4008]{0,1:T(8,128)(2,1)S(1)}, bf16[128,4008]{0,1:T(8,128)(2,1)}, u32[]{:S(2)}) copy-start(bf16[128,4008]{0,1:T(8,128)(2,1)} %param.7) | copy-start | bytes 3078148
  378.9 56.6 %all-to-all-start.2 = ((bf16[128,32,256]{0,2,1:T(8,128)(2,1)}), bf16[128,32,256]{0,2,1:T(8,128)(2,1)}, u32[]{:S(2)}, u32[]{:S(2)}) async-start(bf16[128,32,256]{0,2,1:T(8,128)(2,1)} %select_select_fusion), calls=%async_computation.2 | async-start | bytes 4194304 | tf_op jit(solution)/shard_map/all_to_all | solution.py:117
Sparse Core Ops, SparseCore 0:
  21.8 42.3 all-gather.9
